TPU v7x, 32 devices: a whole 2x2x4 slice. The times are simulated.
32 devices in a mesh: rep: 4 (over z), head: 4 (over y, core), pair: 2 (over x).
Axes of the slice: x: 2, y: 2, z: 4, core: 2. Of those that a mesh axis runs over, the one named last changes fastest.
Arguments:
- queries: bfloat16 [96, 8192], P(('rep', 'pair'), 'head'), may hold values from -24 to 24
- new_keys: bfloat16 [96, 1024], P(('rep', 'pair'), 'head'), may hold values from -6 to 6
- new_values: bfloat16 [96, 1024], P(('rep', 'pair'), 'head'), may hold values from -6 to 6
- key_cache: bfloat16 [96, 1024, 1024], P(('rep', 'pair'), None, 'head'), may hold values from -6 to 6
- value_cache: bfloat16 [96, 1024, 1024], P(('rep', 'pair'), None, 'head'), may hold values from -6 to 6
- lengths: int32 [96], P(('rep', 'pair')), may hold values from 2 to 1024
- residual: bfloat16 [96, 8192], P('head', ('rep', 'pair')), may hold values from -36 to 36
- norm_gain: float32 [8192], replicated, may hold values from 0.5 to 1.5
- out_weight: bfloat16 [8192, 8192], P('head', ('rep', 'pair')), may hold values from -0.5 to 0.5
- gate_weight: bfloat16 [8192, 28672], P('head', ('rep', 'pair')), may hold values from -0.0625 to 0.0625
- up_weight: bfloat16 [8192, 28672], P('head', ('rep', 'pair')), may hold values from -0.0625 to 0.0625
- down_weight: bfloat16 [28672, 8192], P(('rep', 'pair'), 'head'), may hold values from -0.03125 to 0.03125
Outputs:
- hidden_state: bfloat16 [96, 8192], P('head', ('rep', 'pair'))
- ffn_out: bfloat16 [96, 8192], P(('rep', 'pair'), 'head')
Inputs may be any that keep to these rules, and one draw needn't show every extreme that they name: Cache slots 0 to lengths - 1 of a row are live, the others are ignored.
All inputs are finite; a program needn't handle non-finite values.
Results may differ from a plain program's by a relative error of at most 0.0095.
Values may be sent and summed in bfloat16 or wider, within the bound.
A program may use at most 128 MiB of HBM per device.

v0:
```python
import jax
import jax.numpy as jnp
from jax import lax
from jax.sharding import PartitionSpec as P

HEADS = 64
KV_HEADS = 8
HEAD_DIM = 128


def local(
    queries,
    new_keys,
    new_values,
    key_cache,
    value_cache,
    lengths,
    residual,
    norm_gain,
    out_weight,
    gate_weight,
    up_weight,
    down_weight,
):
    row_count = queries.shape[0]
    slot_count = key_cache.shape[1]
    kv_local = key_cache.shape[2] // HEAD_DIM
    group_size = HEADS // KV_HEADS
    score_scale = HEAD_DIM ** (-0.5)
    query_heads = queries.reshape(row_count, kv_local, group_size, HEAD_DIM)
    cached_keys = key_cache.reshape(row_count, slot_count, kv_local, HEAD_DIM)
    cached_values = value_cache.reshape(row_count, slot_count, kv_local, HEAD_DIM)
    key_new = new_keys.reshape(row_count, kv_local, HEAD_DIM)
    value_new = new_values.reshape(row_count, kv_local, HEAD_DIM).astype(jnp.float32)
    scores = (
        jnp.einsum("rhgd,rchd->rhgc", query_heads, cached_keys, preferred_element_type=jnp.float32)
        * score_scale
    )
    slot_ids = lax.broadcasted_iota(jnp.int32, (row_count, 1, 1, slot_count), 3)
    live_mask = slot_ids < lengths[:, None, None, None]
    scores = jnp.where(live_mask, scores, -jnp.inf)
    own_score = (
        jnp.einsum("rhgd,rhd->rhg", query_heads, key_new, preferred_element_type=jnp.float32)
        * score_scale
    )
    row_top = jnp.maximum(jnp.max(scores, axis=3), own_score)
    weights = jnp.exp(scores - row_top[..., None])
    own_weight = jnp.exp(own_score - row_top)
    weight_total = jnp.sum(weights, axis=3) + own_weight
    weights_low = weights.astype(jnp.bfloat16)
    own_low = own_weight.astype(jnp.bfloat16).astype(jnp.float32)
    mixture = jnp.einsum(
        "rhgc,rchd->rhgd", weights_low, cached_values, preferred_element_type=jnp.float32
    )
    mixture = mixture + own_low[..., None] * value_new[:, :, None, :]
    attn = (mixture / weight_total[..., None]).astype(jnp.bfloat16).reshape(row_count, -1)
    projected_terms = jnp.dot(
        lax.all_gather(attn, ("rep", "pair"), axis=0, tiled=True),
        out_weight,
        preferred_element_type=jnp.float32,
    )
    projected = lax.psum_scatter(projected_terms, "head", scatter_dimension=0, tiled=True)
    hidden_state = (residual.astype(jnp.float32) + projected).astype(jnp.bfloat16)
    full_rows = lax.all_gather(hidden_state, ("rep", "pair"), axis=1, tiled=True)
    state_f = full_rows.astype(jnp.float32)
    mean_square = jnp.mean(state_f * state_f, axis=1, keepdims=True)
    normed = (state_f * lax.rsqrt(mean_square + 1e-05) * norm_gain).astype(jnp.bfloat16)
    normed_cols = lax.all_to_all(normed, "head", split_axis=1, concat_axis=0, tiled=True)
    gate_part = jnp.dot(normed_cols, gate_weight, preferred_element_type=jnp.float32)
    up_part = jnp.dot(normed_cols, up_weight, preferred_element_type=jnp.float32)
    gate_share, up_share = (
        lax.psum_scatter(gate_part, "head", scatter_dimension=1, tiled=True),
        lax.psum_scatter(up_part, "head", scatter_dimension=1, tiled=True),
    )
    hidden_share = (jax.nn.silu(gate_share) * up_share).astype(jnp.bfloat16)
    hidden = lax.all_gather(hidden_share, "head", axis=1, tiled=True)
    ffn_out = lax.psum_scatter(
        jnp.dot(hidden, down_weight, preferred_element_type=jnp.float32),
        ("rep", "pair"),
        scatter_dimension=0,
        tiled=True,
    )
    return (hidden_state, ffn_out.astype(jnp.bfloat16))


def solution(mesh):
    placed = (
        P(("rep", "pair"), "head"),
        P(("rep", "pair"), "head"),
        P(("rep", "pair"), "head"),
        P(("rep", "pair"), None, "head"),
        P(("rep", "pair"), None, "head"),
        P(("rep", "pair")),
        P("head", ("rep", "pair")),
        P(),
        P("head", ("rep", "pair")),
        P("head", ("rep", "pair")),
        P("head", ("rep", "pair")),
        P(("rep", "pair"), "head"),
    )
    return jax.shard_map(
        local,
        mesh=mesh,
        in_specs=placed,
        out_specs=(P("head", ("rep", "pair")), P(("rep", "pair"), "head")),
        check_vma=False,
    )
```

profile of v0, /device:TPU:10, one launch (start us, length us, event | category | flops | bytes accessed | tf_op | source)
XLA Modules:
  0.0 246.1 jit_solution(1456048309549870125)
XLA Ops:
  7.2 0.0 copy-start.3
  7.2 0.0 reduce-scatter.6.cloned.1.call-start
  7.2 0.9 copy.27
  8.1 0.7 iota_compare_fusion
  8.8 0.7 reshape.72
  9.5 0.1 fusion.29
  9.7 4.6 %fusion.35 = (f32[12,2,8]{2,1,0:T(2,128)S(1)}, f32[12,2,8,1024]{3,2,1,0:T(8,128)S(1)}) fusion(bf16[16,16,128]{2,1,0:T(8,128)(2,1)S(1)} %bitcast.64, pred[12,1024]{1,0:T(8,128)(4,1)S(1)} %iota_compare_fusion, bf16[12,1024,256]{2,1,0:T(8,128)(2,1)} %param.15), kind=kOutput, calls=%fused_computation.35 | convolution fusion | flops 50921280 | bytes 7144192 | tf_op jit(solution)/shard_map/rhgd,rchd->rhgc/dot_general | solution.py:36
  14.3 0.3 fusion.25
  14.6 0.0 copy-done.3
  14.6 0.0 copy-start.1
  14.7 0.0 copy-start.2
  14.7 3.8 %fusion.19 = bf16[12,2,8,128]{3,2,1,0:T(8,128)(2,1)S(1)} fusion(f32[12,2,8,1024]{3,2,1,0:T(8,128)S(1)} %get-tuple-element.5, f32[12,2,8]{2,1,0:T(2,128)S(1)} %multiply_maximum_fusion, f32[12,2,8]{2,1,0:T(2,128)S(1)} %get-tuple-element.3, f32[12,2,128]{2,1,0:T(2,128)S(1)} %reshape.65, f32[12,2,8]{2,1,0:T(2,128)S(1)} %get-tuple-element.2, ...), kind=kOutput, calls=%fused_computation.10 | convolution fusion | flops 50823168 | bytes 7141632 | tf_op jit(solution)/shard_map/rhgc,rchd->rhgd/dot_general | solution.py:52
  18.5 0.1 reshape.66
  18.5 29.5 %all-gather = bf16[8,12,2048]{2,1,0:T(8,128)(2,1)S(1)} all-gather(bf16[1,12,2048]{2,1,0:T(8,128)(2,1)S(1)} %reshape.66), channel_id=1, replica_groups=mesh['rep'=4,'head'=4,'pair'=2] {'rep','pair'}, dimensions={0}, use_global_device_ids=true | all-gather | bytes 442368 | tf_op jit(solution)/shard_map/all_gather | solution.py:58
  48.0 0.1 reshape.67
  48.1 3.7 %fusion.36 = f32[96,1024]{1,0:T(8,128)} fusion(bf16[96,2048]{1,0:T(8,128)(2,1)S(1)} %reshape.67, bf16[2048,1024]{1,0:T(8,128)(2,1)} %param.20), kind=kOutput, calls=%fused_computation.36 | convolution fusion | flops 402653184 | bytes 4980736 | tf_op jit(solution)/shard_map/dot_general | solution.py:57
  51.8 0.0 reduce-scatter.6.cloned.1.call-update
  51.8 0.0 reduce-scatter.10.cloned.1.call-start
  51.9 24.0 %reduce-scatter.6.cloned.1.call-done = f32[24,1024]{1,0:T(8,128)} async-done(((f32[96,1024]{1,0:T(8,128)}), f32[24,1024]{1,0:T(8,128)}) %reduce-scatter.6.cloned.1.call-update) | async-done | bytes 98320 | tf_op jit(solution)/shard_map/reduce_scatter | solution.py:62
  75.9 0.0 copy-done.1
  75.9 0.9 add_convert_fusion
  76.8 0.0 copy-start
  76.8 28.8 %all_gather.10 = bf16[24,8192]{1,0:T(8,128)(2,1)S(1)} all-gather(bf16[24,1024]{1,0:T(8,128)(2,1)S(1)} %add_convert_fusion), channel_id=1, replica_groups=mesh['rep'=4,'head'=4,'pair'=2] {'rep','pair'}, dimensions={1}, use_global_device_ids=true | all-gather | bytes 442368 | tf_op jit(solution)/shard_map/all_gather | solution.py:64
  105.6 0.2 fusion.22
  105.8 0.0 copy-done.2
  105.9 0.2 fusion.24
  106.1 9.8 %all_to_all.19 = bf16[24,4,2048]{2,0,1:T(8,128)(2,1)S(1)} all-to-all(bf16[24,4,2048]{2,0,1:T(8,128)(2,1)S(1)} %bitcast.62), channel_id=1, replica_groups=mesh['rep'=4,'head'=4,'pair'=2] {'head'}, dimensions={1} | all-to-all | bytes 786432 | tf_op jit(solution)/shard_map/all_to_all | solution.py:68
  115.9 8.7 %fusion.38 = f32[96,3584]{1,0:T(8,128)} fusion(bf16[96,2048]{1,0:T(8,128)(2,1)S(1)} %bitcast.59, bf16[2048,3584]{1,0:T(8,128)(2,1)} %param.22), kind=kOutput, calls=%fused_computation.38 | convolution fusion | flops 1409286144 | bytes 16449536 | tf_op jit(solution)/shard_map/dot_general | solution.py:70
  124.5 0.0 copy-done
  124.5 0.0 reduce-scatter.10.cloned.1.call-update
  124.6 0.0 reduce-scatter.8.cloned.1.call-start
  124.6 8.7 %fusion.37 = f32[96,3584]{1,0:T(8,128)} fusion(bf16[96,2048]{1,0:T(8,128)(2,1)S(1)} %bitcast.60, bf16[2048,3584]{1,0:T(8,128)(2,1)} %param.21), kind=kOutput, calls=%fused_computation.37 | convolution fusion | flops 1409286144 | bytes 16449536 | tf_op jit(solution)/shard_map/dot_general | solution.py:69
  133.3 0.0 reduce-scatter.8.cloned.1.call-update
  133.4 20.6 %reduce-scatter.10.cloned.1.call-done = f32[96,896]{1,0:T(8,128)} async-done(((f32[96,3584]{1,0:T(8,128)}), f32[96,896]{1,0:T(8,128)}) %reduce-scatter.10.cloned.1.call-update) | async-done | bytes 344080 | tf_op jit(solution)/shard_map/reduce_scatter | solution.py:73
  154.0 29.4 %reduce-scatter.8.cloned.1.call-done = f32[96,896]{1,0:T(8,128)} async-done(((f32[96,3584]{1,0:T(8,128)}), f32[96,896]{1,0:T(8,128)}) %reduce-scatter.8.cloned.1.call-update) | async-done | bytes 344080 | tf_op jit(solution)/shard_map/reduce_scatter | solution.py:72
  183.4 1.2 multiply_convert_fusion
  184.6 7.5 %all_gather.11 = bf16[96,3584]{1,0:T(8,128)(2,1)S(1)} all-gather(bf16[96,896]{1,0:T(8,128)(2,1)S(1)} %multiply_convert_fusion), channel_id=1, replica_groups=mesh['rep'=4,'head'=4,'pair'=2] {'head'}, dimensions={1}, use_global_device_ids=true | all-gather | bytes 860160 | tf_op jit(solution)/shard_map/all_gather | solution.py:76
  192.1 0.0 copy-start.4
  192.1 7.8 %fusion.39 = f32[96,2048]{1,0:T(8,128)S(1)} fusion(bf16[96,3584]{1,0:T(8,128)(2,1)S(1)} %all_gather.11, bf16[3584,2048]{1,0:T(8,128)(2,1)} %param.23), kind=kOutput, calls=%fused_computation.39 | convolution fusion | flops 1409286144 | bytes 16154624 | tf_op jit(solution)/shard_map/dot_general | solution.py:78
  199.9 27.8 %fusion = f32[16,2048]{1,0:T(8,128)S(1)} fusion(f32[96,2048]{1,0:T(8,128)S(1)} %fusion.39), kind=kCustom, calls=%all-reduce-scatter | all-reduce-scatter fusion | flops 262145 | bytes 918016
  227.7 4.6 %collective-permute-start = (bf16[16,2048]{1,0:T(8,128)(2,1)S(1)}, bf16[16,2048]{1,0:T(8,128)(2,1)S(1)}, u32[]{:S(2)}, u32[]{:S(2)}) collective-permute-start(bf16[16,2048]{1,0:T(8,128)(2,1)S(1)} %convert.1), channel_id=1, source_target_pairs={{0,1},{1,8},{8,9},{9,16},{16,17},{17,24},{24,25},{2,3},{3,10},{10,... | collective-permute-start | bytes 196616
  232.3 2.5 %collective-permute-start.1 = (bf16[12,2048]{1,0:T(8,128)(2,1)S(1)}, bf16[12,2048]{1,0:T(8,128)(2,1)S(1)}, u32[]{:S(2)}, u32[]{:S(2)}) collective-permute-start(bf16[12,2048]{1,0:T(8,128)(2,1)S(1)} %slice), channel_id=1, source_target_pairs={{0,8},{1,9},{8,16},{9,17},{16,24},{17,25},{2,10},{3,11},{10,18},{1... | collective-permute-start | bytes 147464
  234.8 0.0 copy-done.4
  234.9 0.6 dynamic-slice.4
  236.1 2.4 collective-permute-done.1
  238.5 0.0 collective-permute-done
  238.5 0.4 concatenate
  238.9 0.7 dynamic-slice_convert_fusion
  (7 shorter events, 0.1 us)
Async XLA Ops:
  7.2 7.5 %copy-start.3 = (bf16[12,256]{1,0:T(8,128)(2,1)S(1)}, bf16[12,256]{1,0:T(8,128)(2,1)}, u32[]{:S(2)}) copy-start(bf16[12,256]{1,0:T(8,128)(2,1)} %param.14) | copy-start | bytes 18436
  7.2 68.7 %reduce-scatter.6.cloned.1.call-start = ((), (), s32[]{:S(2)}) async-start(), calls=%async_computation.4 | async-start | bytes 491520 | tf_op jit(solution)/shard_map/reduce_scatter | solution.py:62
  14.6 61.2 %copy-start.1 = (bf16[24,1024]{1,0:T(8,128)(2,1)S(1)}, bf16[24,1024]{1,0:T(8,128)(2,1)}, u32[]{:S(2)}) copy-start(bf16[24,1024]{1,0:T(8,128)(2,1)} %param.18) | copy-start | bytes 147460
  14.7 91.2 %copy-start.2 = (f32[8192]{0:T(1024)S(1)}, f32[8192]{0:T(1024)}, u32[]{:S(2)}) copy-start(f32[8192]{0:T(1024)} %param.19) | copy-start | bytes 98308
  51.8 102.1 %reduce-scatter.10.cloned.1.call-start = ((), (), s32[]{:S(2)}) async-start(), calls=%async_computation.6 | async-start | bytes 1720320 | tf_op jit(solution)/shard_map/reduce_scatter | solution.py:73
  76.8 47.8 %copy-start = (bf16[24,1024]{1,0:T(8,128)(2,1)}, bf16[24,1024]{1,0:T(8,128)(2,1)S(1)}, u32[]{:S(2)}) copy-start(bf16[24,1024]{1,0:T(8,128)(2,1)S(1)} %add_convert_fusion) | copy-start | bytes 147460
  124.6 58.8 %reduce-scatter.8.cloned.1.call-start = ((), (), s32[]{:S(2)}) async-start(), calls=%async_computation.5 | async-start | bytes 1720320 | tf_op jit(solution)/shard_map/reduce_scatter | solution.py:72
  192.1 42.8 %copy-start.4 = (u32[32]{0:T(128)S(1)}, u32[32]{0:T(128)}, u32[]{:S(2)}) copy-start(u32[32]{0:T(128)} %constant.23) | copy-start | bytes 388
  227.7 10.8 %collective-permute-start = (bf16[16,2048]{1,0:T(8,128)(2,1)S(1)}, bf16[16,2048]{1,0:T(8,128)(2,1)S(1)}, u32[]{:S(2)}, u32[]{:S(2)}) collective-permute-start(bf16[16,2048]{1,0:T(8,128)(2,1)S(1)} %convert.1), channel_id=1, source_target_pairs={{0,1},{1,8},{8,9},{9,16},{16,17},{17,24},{24,25},{2,3},{3,10},{10,... | collective-permute-start | bytes 196616
  232.3 6.2 %collective-permute-start.1 = (bf16[12,2048]{1,0:T(8,128)(2,1)S(1)}, bf16[12,2048]{1,0:T(8,128)(2,1)S(1)}, u32[]{:S(2)}, u32[]{:S(2)}) collective-permute-start(bf16[12,2048]{1,0:T(8,128)(2,1)S(1)} %slice), channel_id=1, source_target_pairs={{0,8},{1,9},{8,16},{9,17},{16,24},{17,25},{2,10},{3,11},{10,18},{1... | collective-permute-start | bytes 147464
Sparse Core Ops, SparseCore 0:
  52.0 23.8 reduce-scatter.5
  124.7 29.2 reduce-scatter.9
  156.5 26.8 reduce-scatter.7
where the time goes:
time: 247 us; the launch traced here: 246 us
  blocking collectives  103 us (42%)
  waiting for transfers between devices  76.5 us (31%)
  matrix products  37.5 us (15%)
  between operations  14.6 us (6%)
  starting transfers between devices  7.25 us (3%)
  other arithmetic  3.53 us (1%)
  local copies, waits for them, and re-layouts  3.42 us (1%)
    all_gather x1, blocking collectives, local(): lax.all_gather(attn, ('rep', 'pair'), axis=0, tiled=True)  29.5 us
    reduce_scatter x1, waiting for transfers between devices, local(): lax.psum_scatter(gate_part, 'head', scatter_dimension=1, tiled=True)  29.4 us
    all_gather x1, blocking collectives, local(): lax.all_gather(hidden_state, ('rep', 'pair'), axis=1, tiled=True)  28.8 us
    unnamed x1, blocking collectives  27.8 us
    reduce_scatter x1, waiting for transfers between devices, local(): lax.psum_scatter(projected_terms, 'head', scatter_dimension=0, tiled=True)  24 us
    reduce_scatter x1, waiting for transfers between devices, local(): lax.psum_scatter(up_part, 'head', scatter_dimension=1, tiled=True)  20.6 us
    all_to_all x1, blocking collectives, local(): lax.all_to_all(normed, 'head', split_axis=1, concat_axis=0, tiled=True)  9.8 us
    dot_general x1, matrix products, local(): jnp.dot(normed_cols, gate_weight, preferred_element_type=jnp.float32)  8.72 us
  transfers between devices with their start and end apart: 5, of which 4 were waited for; matrix products, arithmetic and copies ran while one was open for 4% of the time, Pallas kernels for 0%

commit v1 on v0

v1 whole, which is shorter than its diff:
```python
import functools

import jax
import jax.numpy as jnp
from jax import lax
from jax.experimental import pallas as pl
from jax.experimental.pallas import tpu as pltpu
from jax.sharding import PartitionSpec as P

HEADS = 64
KV_HEADS = 8
HEAD_DIM = 128
CHUNKS = 7
SLOTS = 4
MESH = pl.DeviceIdType.MESH
F32 = jnp.float32
BF16 = jnp.bfloat16


def kernel(
    R, H, PR,
    len_ref, q_ref, nk_ref, nv_ref, res_ref, gain_ref,
    k_hbm, v_hbm, ow_hbm, gw_hbm, uw_hbm, dw_hbm,
    hid_out, ffn_out,
    kbuf, vbuf, ow, gw, uw, dw,
    qs, nk32, nv32, ao, agb, pb, bsend, brecv, hsb, cb, xs, xbf,
    ss_send, ss_recv, rscale, dsend, drecv, eb, hx, acc, fsend, frecv,
    kv_sem, w_sem,
    a_s, a_r, b_s, b_r, c_s, c_r, s_s, s_r, d_s, d_r, e_s, e_r, f_s, f_r,
):
    G = R * PR
    gpb = G // H
    rep = lax.axis_index("rep")
    h = lax.axis_index("head")
    pair = lax.axis_index("pair")
    g = rep * PR + pair
    b = q_ref.shape[0]
    slots = kbuf.shape[1]
    kvl = kbuf.shape[2] // HEAD_DIM
    grp = HEADS // KV_HEADS
    nq = kvl * grp
    rb = hsb.shape[0]
    cb_cols = hsb.shape[1]
    C = gw.shape[2]
    D = gain_ref.shape[1]
    scale = HEAD_DIM ** (-0.5)

    def kcopy(r):
        s = lax.rem(r, SLOTS)
        return pltpu.make_async_copy(k_hbm.at[r], kbuf.at[s], kv_sem.at[0, s])

    def vcopy(r):
        s = lax.rem(r, SLOTS)
        return pltpu.make_async_copy(v_hbm.at[r], vbuf.at[s], kv_sem.at[1, s])

    def ow_copy():
        return pltpu.make_async_copy(ow_hbm, ow, w_sem.at[3, 0])

    def g_copy(c):
        return pltpu.make_async_copy(
            gw_hbm.at[:, pl.ds(pl.multiple_of(c * C, C), C)], gw.at[c], w_sem.at[0, c])

    def u_copy(c):
        return pltpu.make_async_copy(
            uw_hbm.at[:, pl.ds(pl.multiple_of(c * C, C), C)], uw.at[c], w_sem.at[1, c])

    def d_copy(c):
        return pltpu.make_async_copy(
            dw_hbm.at[pl.ds(pl.multiple_of(c * C, C), C), :], dw.at[c], w_sem.at[2, c])

    def to_group(src, dst, ss, rs, gd):
        return pltpu.make_async_remote_copy(
            src_ref=src, dst_ref=dst, send_sem=ss, recv_sem=rs,
            device_id=(gd // PR, h, lax.rem(gd, PR)), device_id_type=MESH)

    def to_head(src, dst, ss, rs, hd):
        return pltpu.make_async_remote_copy(
            src_ref=src, dst_ref=dst, send_sem=ss, recv_sem=rs,
            device_id=(rep, hd, pair), device_id_type=MESH)

    for r in range(min(SLOTS, b)):
        kcopy(r).start()
        vcopy(r).start()
    ow_copy().start()
    for i in range(nq):
        qs[pl.ds(i, b, stride=nq), :] = q_ref[:, i * HEAD_DIM:(i + 1) * HEAD_DIM].astype(F32)
    nk32[...] = nk_ref[...].astype(F32)
    nv32[...] = nv_ref[...].astype(F32)

    def attend(r, _):
        s = lax.rem(r, SLOTS)
        kcopy(r).wait()
        q16 = qs[pl.ds(pl.multiple_of(r * nq, nq), nq), :]
        own_of = lax.broadcasted_iota(jnp.int32, (nq, HEAD_DIM), 0) // grp
        qbd = jnp.concatenate(
            [jnp.where(own_of == j, q16, 0.0) for j in range(kvl)], axis=1) if kvl > 1 else q16
        sc = lax.dot_general(
            qbd.astype(BF16), kbuf[s], (((1,), (1,)), ((), ())), preferred_element_type=F32) * scale
        ids = lax.broadcasted_iota(jnp.int32, (nq, slots), 1)
        sc = jnp.where(ids < len_ref[r], sc, -jnp.inf)
        own = jnp.sum(qbd * nk32[pl.ds(r, 1), :], axis=1, keepdims=True) * scale
        top = jnp.maximum(jnp.max(sc, axis=1, keepdims=True), own)
        w = jnp.exp(sc - top)
        ownw = jnp.exp(own - top)
        tot = jnp.sum(w, axis=1, keepdims=True) + ownw
        vcopy(r).wait()
        o = jnp.dot(w.astype(BF16), vbuf[s], preferred_element_type=F32)
        o = (o + ownw.astype(BF16).astype(F32) * nv32[pl.ds(r, 1), :]) / tot
        for j in range(kvl):
            ao[pl.ds(pl.multiple_of(r * nq + j * grp, grp), grp), :] = (
                o[j * grp:(j + 1) * grp, j * HEAD_DIM:(j + 1) * HEAD_DIM])

        @pl.when(r + SLOTS < b)
        def _():
            kcopy(r + SLOTS).start()
            vcopy(r + SLOTS).start()

        @pl.when(jnp.logical_and(r >= 3, r < 3 + CHUNKS))
        def _():
            g_copy(r - 3).start()
        return 0

    lax.fori_loop(0, b, attend, 0)
    agb[g] = jnp.zeros(agb.shape[1:], BF16)
    for i in range(nq):
        agb[g, 0:b, i * HEAD_DIM:(i + 1) * HEAD_DIM] = ao[pl.ds(i, b, stride=nq), :].astype(BF16)

    def a_copy(d):
        gd = lax.rem(g + d, G)
        return to_group(agb.at[g], agb.at[g], a_s.at[d], a_r.at[g], gd)

    def a_in(d):
        gs = lax.rem(g + d, G)
        return to_group(agb.at[gs], agb.at[gs], a_s.at[d], a_r.at[gs], gs)

    for d in range(1, G):
        a_copy(d).start()
    for c in range(CHUNKS):
        u_copy(c).start()
    for c in range(CHUNKS):
        d_copy(c).start()
    ow_copy().wait()
    for d in range(1, G):
        a_in(d).wait_recv()

    pad = agb.shape[1]
    full = agb[...].reshape(G * pad, agb.shape[2])
    prod = jnp.dot(full, ow[...], preferred_element_type=F32)
    for a in range(G):
        pb[a * b:(a + 1) * b, :] = prod[a * pad:a * pad + b, :]
    for j in range(H):
        bsend[j] = pb[j * rb:(j + 1) * rb, :].astype(BF16)

    def b_copy(d):
        hd = lax.rem(h + d, H)
        return to_head(bsend.at[hd], brecv.at[h], b_s.at[d], b_r.at[h], hd)

    def b_in(d):
        hs = lax.rem(h + d, H)
        return to_head(bsend.at[hs], brecv.at[hs], b_s.at[d], b_r.at[hs], hs)

    for d in range(1, H):
        b_copy(d).start()
    total = res_ref[...].astype(F32) + pb[pl.ds(pl.multiple_of(h * rb, rb), rb), :]
    for d in range(1, H):
        b_in(d).wait_recv()
        total = total + brecv[lax.rem(h + d, H)].astype(F32)
    state = total.astype(BF16)
    hid_out[...] = state
    hsb[...] = state

    hd_c = g // gpb
    slot_c = h * gpb + lax.rem(g, gpb)

    def c_copy(d):
        gd = lax.rem(g + d, G)
        return pltpu.make_async_remote_copy(
            src_ref=hsb, dst_ref=cb.at[slot_c], send_sem=c_s.at[d], recv_sem=c_r.at[slot_c],
            device_id=(gd // PR, hd_c, lax.rem(gd, PR)), device_id_type=MESH)

    for d in range(1, G):
        c_copy(d).start()

    @pl.when(hd_c != h)
    def _():
        c_copy(0).start()

    @pl.when(hd_c == h)
    def _():
        cb[slot_c] = state

    for j in range(H):
        for k in range(gpb):
            mine = jnp.logical_and(h == j, g == h * gpb + k)

            @pl.when(jnp.logical_not(mine))
            def _():
                pltpu.make_async_remote_copy(
                    src_ref=hsb, dst_ref=cb.at[j * gpb + k], send_sem=c_s.at[0],
                    recv_sem=c_r.at[j * gpb + k], device_id=(rep, lax.rem(h + 1, H), pair),
                    device_id_type=MESH).wait_recv()

    for j in range(H):
        sq = jnp.zeros((rb, 1), F32)
        for k in range(gpb):
            xv = cb[j * gpb + k].astype(F32)
            sq = sq + jnp.sum(xv * xv, axis=1, keepdims=True)
            gain = gain_ref[:, pl.ds(pl.multiple_of((h * gpb + k) * cb_cols, cb_cols), cb_cols)]
            xs[j * rb:(j + 1) * rb, k * cb_cols:(k + 1) * cb_cols] = xv * gain
        ss_send[j] = jnp.broadcast_to(sq, (rb, 128))
    xbf[...] = xs[...].astype(BF16)

    def s_copy(d):
        hd = lax.rem(h + d, H)
        return to_head(ss_send.at[hd], ss_recv.at[h], s_s.at[d], s_r.at[h], hd)

    def s_in(d):
        hs = lax.rem(h + d, H)
        return to_head(ss_send.at[hs], ss_recv.at[hs], s_s.at[d], s_r.at[hs], hs)

    for d in range(1, H):
        s_copy(d).start()

    def d_out(c, d):
        hd = lax.rem(h + d, H)
        return to_head(dsend.at[c, hd], drecv.at[c, h], d_s.at[c, d], d_r.at[c, h], hd)

    def d_in(c, d):
        hs = lax.rem(h + d, H)
        return to_head(dsend.at[c, hs], drecv.at[c, hs], d_s.at[c, d], d_r.at[c, hs], hs)

    def e_out(c, d):
        hd = lax.rem(h + d, H)
        return to_head(eb.at[c, h], eb.at[c, h], e_s.at[c, d], e_r.at[c, h], hd)

    def e_in(c, d):
        hs = lax.rem(h + d, H)
        return to_head(eb.at[c, hs], eb.at[c, hs], e_s.at[c, d], e_r.at[c, hs], hs)

    def expand(c):
        for m, (copy, wt) in enumerate(((g_copy, gw), (u_copy, uw))):
            copy(c).wait()
            part = jnp.dot(xbf[...], wt[c], preferred_element_type=F32)
            for j in range(H):
                dsend[c, j, :, m * C:(m + 1) * C] = part[j * rb:(j + 1) * rb, :].astype(BF16)
        for d in range(1, H):
            d_out(c, d).start()

    def activate(c):
        both = dsend[c, h].astype(F32)
        for d in range(1, H):
            d_in(c, d).wait_recv()
            both = both + drecv[c, lax.rem(h + d, H)].astype(F32)
        both = both * rscale[:, 0:1]
        gate = both[:, :C]
        up = both[:, C:]
        eb[c, h] = (gate / (1.0 + jnp.exp(-gate)) * up).astype(BF16)
        for d in range(1, H):
            e_out(c, d).start()

    def contract(c):
        d_copy(c).wait()
        for d in range(1, H):
            e_in(c, d).wait_recv()
        for j in range(H):
            hx[j * rb:(j + 1) * rb, :] = eb[c, j].astype(F32)
        acc[...] += jnp.dot(hx[...].astype(BF16), dw[c], preferred_element_type=F32)

    acc[...] = jnp.zeros_like(acc)
    lag1, lag2 = 2, 4

    def stage(t, _):
        @pl.when(t < CHUNKS)
        def _():
            expand(t)

        @pl.when(t == lag1 - 1)
        def _():
            sq = ss_send[h]
            for d in range(1, H):
                s_in(d).wait_recv()
                sq = sq + ss_recv[lax.rem(h + d, H)]
            rscale[...] = lax.rsqrt(sq * (1.0 / D) + 1e-05)

        @pl.when(jnp.logical_and(t >= lag1, t < CHUNKS + lag1))
        def _():
            activate(t - lag1)

        @pl.when(t >= lag2)
        def _():
            contract(t - lag2)
        return 0

    lax.fori_loop(0, CHUNKS + lag2, stage, 0)

    for a in range(G):
        fsend[a] = acc[a * b:(a + 1) * b, :].astype(BF16)

    def f_copy(d):
        gd = lax.rem(g + d, G)
        return to_group(fsend.at[gd], frecv.at[g], f_s.at[d], f_r.at[g], gd)

    def f_in(d):
        gs = lax.rem(g + d, G)
        return to_group(fsend.at[gs], frecv.at[gs], f_s.at[d], f_r.at[gs], gs)

    for d in range(1, G):
        f_copy(d).start()
    out = fsend[g].astype(F32)
    for d in range(1, G):
        f_in(d).wait_recv()
        out = out + frecv[lax.rem(g + d, G)].astype(F32)
    ffn_out[...] = out.astype(BF16)

    for d in range(1, G):
        a_copy(d).wait_send()
        c_copy(d).wait_send()
        f_copy(d).wait_send()

    @pl.when(hd_c != h)
    def _():
        c_copy(0).wait_send()

    for d in range(1, H):
        b_copy(d).wait_send()
        s_copy(d).wait_send()

    def drain(c, _):
        for d in range(1, H):
            d_out(c, d).wait_send()
            e_out(c, d).wait_send()
        return 0

    lax.fori_loop(0, CHUNKS, drain, 0)


def local(
    R, H, PR,
    queries, new_keys, new_values, key_cache, value_cache, lengths,
    residual, norm_gain, out_weight, gate_weight, up_weight, down_weight,
):
    G = R * PR
    b, qw = queries.shape
    kvw = new_keys.shape[1]
    slots = key_cache.shape[1]
    rb, oc = residual.shape
    D = norm_gain.shape[0]
    fin, units = gate_weight.shape
    dout = down_weight.shape[1]
    C = units // CHUNKS
    B = b * G
    nq = qw // HEAD_DIM
    pad = -(-b // 16) * 16
    gpb = G // H
    V, S = pltpu.VMEM, pltpu.SemaphoreType.DMA
    vm = pl.BlockSpec(memory_space=pltpu.VMEM)
    hb = pl.BlockSpec(memory_space=pl.ANY)
    return pl.pallas_call(
        functools.partial(kernel, R, H, PR),
        out_shape=(
            jax.ShapeDtypeStruct((rb, oc), BF16),
            jax.ShapeDtypeStruct((b, dout), BF16),
        ),
        in_specs=[pl.BlockSpec(memory_space=pltpu.SMEM)] + [vm] * 5 + [hb] * 6,
        out_specs=(vm, vm),
        scratch_shapes=[
            V((SLOTS, slots, kvw), BF16), V((SLOTS, slots, kvw), BF16),
            V(out_weight.shape, BF16),
            V((CHUNKS, fin, C), BF16), V((CHUNKS, fin, C), BF16), V((CHUNKS, C, dout), BF16),
            V((b * nq, HEAD_DIM), F32), V((b, kvw), F32), V((b, kvw), F32),
            V((b * nq, HEAD_DIM), F32), V((G, pad, qw), BF16),
            V((B, oc), F32), V((H, rb, oc), BF16), V((H, rb, oc), BF16),
            V((rb, oc), BF16), V((H * gpb, rb, oc), BF16),
            V((B, fin), F32), V((B, fin), BF16),
            V((H, rb, 128), F32), V((H, rb, 128), F32), V((rb, 128), F32),
            V((CHUNKS, H, rb, 2 * C), BF16), V((CHUNKS, H, rb, 2 * C), BF16),
            V((CHUNKS, H, rb, C), BF16), V((B, C), F32), V((B, dout), F32),
            V((G, b, dout), BF16), V((G, b, dout), BF16),
            S((2, SLOTS)), S((4, CHUNKS)),
            S((G,)), S((G,)), S((H,)), S((H,)), S((G,)), S((H * gpb,)), S((H,)), S((H,)),
            S((CHUNKS, H)), S((CHUNKS, H)), S((CHUNKS, H)), S((CHUNKS, H)), S((G,)), S((G,)),
        ],
        compiler_params=pltpu.CompilerParams(
            has_side_effects=True, vmem_limit_bytes=66_900_000),
        name="decode_step",
    )(
        lengths, queries, new_keys, new_values, residual, norm_gain.reshape(1, D),
        key_cache, value_cache, out_weight, gate_weight, up_weight, down_weight,
    )


def solution(mesh):
    placed = (
        P(("rep", "pair"), "head"),
        P(("rep", "pair"), "head"),
        P(("rep", "pair"), "head"),
        P(("rep", "pair"), None, "head"),
        P(("rep", "pair"), None, "head"),
        P(("rep", "pair")),
        P("head", ("rep", "pair")),
        P(),
        P("head", ("rep", "pair")),
        P("head", ("rep", "pair")),
        P("head", ("rep", "pair")),
        P(("rep", "pair"), "head"),
    )
    return jax.shard_map(
        functools.partial(local, mesh.shape["rep"], mesh.shape["head"], mesh.shape["pair"]),
        mesh=mesh,
        in_specs=placed,
        out_specs=(P("head", ("rep", "pair")), P(("rep", "pair"), "head")),
        check_vma=False,
    )
```

time: 247 us -> 88.4 us (0.36)
  blocking collectives: 103 us -> 0 us
  Pallas kernels: 0 us -> 83.9 us
  waiting for transfers between devices: 76.5 us -> 0 us
  matrix products: 37.5 us -> 0 us
  between operations: 14.6 us -> 0.64 us
  starting transfers between devices: 7.25 us -> 0 us
  other arithmetic: 3.53 us -> 0 us
    pallas_call x0 -> x1, Pallas kernels: none -> 83.9 us  [local(): pl.pallas_call(functools.partial(kernel, R, H, PR), out_shape=(jax.ShapeD...]
    reduce_scatter x3 -> x0, waiting for transfers between devices: 74 us -> none  [the longest x1 29.4 us: local(): lax.psum_scatter(gate_part, 'head', scatter_dimension=1, tiled=True)]
    all_gather x3 -> x0, blocking collectives: 65.8 us -> none  [the longest x1 29.5 us: local(): lax.all_gather(attn, ('rep', 'pair'), axis=0, tiled=True)]
    dot_general x7 -> x0, matrix products: 37.5 us -> none  [the longest x1 8.72 us: local(): jnp.dot(normed_cols, gate_weight, preferred_element_type=jnp.float32)]
    unnamed x1 -> x0, blocking collectives: 27.8 us -> none
    all_to_all x1 -> x0, blocking collectives: 9.8 us -> none  [local(): lax.all_to_all(normed, 'head', split_axis=1, concat_axis=0, tiled=True)]
    unnamed x2 -> x0, starting transfers between devices: 7.13 us -> none
  transfers between devices with their start and end apart: 5 -> 0, of which waited for: 4 -> 0; matrix products, arithmetic and copies ran while one was open for 4% -> 0% of each run, Pallas kernels for 0% -> 0%
where the time goes in v1:
time: 88.4 us; the launch traced here: 87.4 us
  Pallas kernels  83.9 us (95%)
  local copies, waits for them, and re-layouts  2.89 us (3%)
    pallas_call x1, Pallas kernels, local(): pl.pallas_call(functools.partial(kernel, R, H, PR), out_shape=(jax.ShapeD...  83.9 us
    unnamed x2, local copies, waits for them, and re-layouts  2.89 us

profile of v1, /device:TPU:10, one launch (start us, length us, event | category | flops | bytes accessed | tf_op | source)
XLA Modules:
  0.0 87.4 jit_solution(13580954622481719488)
XLA Ops:
  0.6 83.9 %decode_step.1 = (bf16[24,1024]{1,0:T(8,128)(2,1)}, bf16[12,2048]{1,0:T(8,128)(2,1)}) custom-call(s32[12]{0:T(128)} %len_ref.1, bf16[12,2048]{1,0:T(8,128)(2,1)} %q_ref.1, bf16[12,256]{1,0:T(8,128)(2,1)} %nk_ref.1, bf16[12,256]{1,0:T(8,128)(2,1)} %nv_ref.1, bf16[24,1024]{1,0:T(8,128)(2,1)} %res_ref.1, f32[1,8192]{1,0:T(1,128)} %bitcast.1, ...), custom_call_target="tpu_custom_call" | custom-call | tf_op jit(solution)/shard_map/decode_step/pallas_call | solution.py:358
  84.5 1.4 %copy.16 = bf16[24,1024]{1,0:T(8,128)(2,1)} copy(bf16[24,1024]{1,0:T(8,128)(2,1)} %get-tuple-element.4) | data formatting | bytes 98304
  86.0 1.5 %copy.17 = bf16[12,2048]{1,0:T(8,128)(2,1)} copy(bf16[12,2048]{1,0:T(8,128)(2,1)} %get-tuple-element.5) | data formatting | bytes 98304
